TPU v7x, 32 devices: a whole 2x2x4 slice. The times are simulated.
32 devices in a mesh: wide: 8 (over z, x), narrow: 4 (over y, core).
Axes of the slice: x: 2, y: 2, z: 4, core: 2. Of those that a mesh axis runs over, the one named last changes fastest.
Arguments:
- hidden: bfloat16 [512, 4, 8192], P('narrow', None, 'wide'), may hold values from -0.1796875 to 0.1796875
- grad_out: bfloat16 [512, 8192], P('narrow', 'wide'), may hold values from -6 to 6
- weight_base: bfloat16 [32768, 8192], P('narrow', 'wide'), may hold values from -0.0625 to 0.0625
- block_scale: bfloat16 [2048, 512], P('narrow', 'wide'), may hold values from 0.25 to 4
Outputs:
- grad_hidden: bfloat16 [512, 4, 8192], P('narrow', None, 'wide')
- grad_weight: bfloat16 [8192, 4, 8192], P('narrow', None, 'wide')
All inputs are finite; a program needn't handle non-finite values.
Results may differ from a plain program's by a relative error of at most 0.0049.
Values may be sent and summed in bfloat16 or wider, within the bound.
A program may use at most 512 MiB of HBM per device.

v0:
```python
import functools

import jax
import jax.numpy as jnp
from jax import lax
from jax.experimental import pallas as pl
from jax.experimental.pallas import tpu as pltpu
from jax.sharding import PartitionSpec as P

MESH = pl.DeviceIdType.MESH
BLOCK = 16
F32 = jnp.float32
BF16 = jnp.bfloat16


def loop(count, body):
    def step(i, carry):
        body(i)
        return carry

    lax.fori_loop(0, count, step, 0)


def add_into(dst, sources, rows):
    def step(i):
        at = pl.ds(pl.multiple_of(i * 16, 16), 16)
        total = sources[0][at, :].astype(F32)
        for source in sources[1:]:
            total = total + source[at, :].astype(F32)
        dst[at, :] = total.astype(BF16)

    loop(rows // 16, step)


def exchange_kernel(
    q, p, ra, scale_ref, weight_ref, grad_ref, hidden_ref,
    gh_ref, cols_ref, hall_ref,
    weff, s32, grads, hid, pa, pb, xr, ud, udb, xrb, fin,
    w_sem, l_sem, ag_s, ag_r, hd_s, hd_r, xa_s, xa_r, ud_s, ud_r, ub_s, ub_r,
    xb_s, xb_r, gh_s, gh_r, mz_s, mz_r, mx_s, mx_r,
):
    wide = q * p
    wi = lax.axis_index("wide")
    n = lax.axis_index("narrow")
    z = wi // p
    x = wi % p
    tokens = grads.shape[1]
    rb = tokens - ra
    high = (2 * z) // q

    def twin(k):
        a, b = n % 2, n // 2
        ka, kb = k % 2, k // 2
        return ((a + ka) % 2) + 2 * ((b + kb) % 2)

    def remote(src, dst, send, recv, to):
        return pltpu.make_async_remote_copy(
            src_ref=src, dst_ref=dst, send_sem=send, recv_sem=recv,
            device_id=to, device_id_type=MESH)

    def at_zx(zz, xx):
        return (zz * p + xx, n)

    def order(i, d):
        return i + (1 - d) * (q - 1 - 2 * i)

    own_grad = pltpu.make_async_copy(grad_ref, grads.at[0], l_sem.at[0])
    own_grad.start()
    own_hid = pltpu.make_async_copy(hidden_ref, hid, l_sem.at[1])
    own_hid.start()

    def weight_copy(c):
        return pltpu.make_async_copy(weight_ref.at[c], weff.at[c], w_sem.at[c])

    def start_weights(i):
        loop(p, lambda xx: weight_copy(order(i, high) * p + xx).start())

    loop(q, start_weights)

    barrier = pltpu.get_barrier_semaphore()

    def greet(device):
        pl.semaphore_signal(barrier, inc=1, device_id=device, device_id_type=MESH)

    for k in range(1, q):
        greet((wi, twin(k)))
    loop(p - 1, lambda r: greet(at_zx(z, (x + 1 + r) % p)))

    @pl.when(z > 0)
    def _():
        greet(at_zx(z - 1, x))

    @pl.when(z < q - 1)
    def _():
        greet(at_zx(z + 1, x))

    ends = (z == 0) | (z == q - 1)

    @pl.when(ends)
    def _():
        pl.semaphore_wait(barrier, q + p - 1)

    @pl.when(jnp.logical_not(ends))
    def _():
        pl.semaphore_wait(barrier, q + p)

    def ag_copy(k):
        return remote(grads.at[0], grads.at[k], ag_s.at[k], ag_r.at[k], (wi, twin(k)))

    def hid_copy(k):
        return remote(hid, hall_ref.at[k], hd_s.at[k], hd_r.at[k], (wi, twin(k)))

    own_grad.wait()
    for k in (2, 3, 1):
        ag_copy(k).start()

    features = weff.shape[2]
    blocks = features // BLOCK
    row = lax.broadcasted_iota(jnp.int32, (blocks, features), 0)
    col = lax.broadcasted_iota(jnp.int32, (blocks, features), 1)
    low = row * BLOCK
    spread = jnp.where((col >= low) & (col < low + BLOCK), 1.0, 0.0).astype(BF16)
    s32[...] = lax.dot_general(
        scale_ref[...], spread, (((0,), (0,)), ((), ())), preferred_element_type=F32)

    own_hid.wait()
    for k in (2, 3, 1):
        hid_copy(k).start()
    hid_here = pltpu.make_async_copy(hid, hall_ref.at[0], l_sem.at[1])
    hid_here.start()

    units = weff.shape[1]
    per_chunk = units // BLOCK

    def scale_chunk(c):
        weight_copy(c).wait()

        def step(i):
            at = pl.ds(pl.multiple_of(i * BLOCK, BLOCK), BLOCK)
            factor = s32[pl.ds(c * per_chunk + i, 1), :]
            weff[c, at, :] = (weff[c, at, :].astype(F32) * factor).astype(BF16)

        loop(per_chunk, step)

    def xa_copy(b, zt, r):
        xx = (x + 1 + r) % p
        return remote(pa.at[b, zt, xx], xr.at[b, zt, r], xa_s.at[b, zt, r], xa_r.at[b, zt, r], at_zx(z, xx))

    def ud_copy(d, b, zt):
        return remote(ud.at[d, b, zt], ud.at[d, b, zt], ud_s.at[d, b, zt], ud_r.at[d, b, zt],
                      at_zx(z + 1 - 2 * d, x))

    def ub_copy(d, b, zt, src):
        return remote(src, udb.at[d, b, zt], ub_s.at[d, b, zt], ub_r.at[d, b, zt],
                      at_zx(z + 1 - 2 * d, x))

    def stage_x(b):
        def per_row(i):
            zt = order(i, high)

            def per_col(xx):
                c = zt * p + xx

                @pl.when(b == 0)
                def _():
                    scale_chunk(c)

                part = lax.dot_general(
                    grads[b], weff[c], (((1,), (1,)), ((), ())), preferred_element_type=F32
                ).astype(BF16)
                pa[b, zt, xx] = part[:ra]
                pb[b, zt, xx] = part[ra:]

            loop(p, per_col)
            loop(p - 1, lambda r: xa_copy(b, zt, r).start())
            for d in range(2):
                @pl.when((z == d * (q - 1)) & (zt != z))
                def _():
                    ub_copy(d, b, zt, pb.at[b, zt]).start()

        loop(q, per_row)

    def wait_x(b, zt):
        loop(p - 1, lambda r: xa_copy(b, zt, r).wait_recv())

    def x_sources(b, zt):
        return [pa.at[b, zt, x]] + [xr.at[b, zt, r] for r in range(p - 1)]

    def stage_z(b):
        for ph in range(2):
            d = (ph + high) % 2
            sign = 1 - 2 * d
            edge = d * (q - 1)

            def step_b(i):
                zt = order(i, d)

                @pl.when(((zt - z) * sign > 0) & (z != edge))
                def _():
                    copy = ub_copy(d, b, zt, udb.at[d, b, zt])
                    copy.wait_recv()
                    loop(p, lambda xx: add_into(
                        udb.at[d, b, zt, xx], [udb.at[d, b, zt, xx], pb.at[b, zt, xx]], rb))
                    copy.start()

            def step_a(i):
                zt = order(i, d)

                @pl.when((zt - z) * sign > 0)
                def _():
                    wait_x(b, zt)
                    copy = ud_copy(d, b, zt)

                    @pl.when(z != edge)
                    def _():
                        copy.wait_recv()
                        add_into(ud.at[d, b, zt], [ud.at[d, b, zt]] + x_sources(b, zt), ra)

                    @pl.when(z == edge)
                    def _():
                        add_into(ud.at[d, b, zt], x_sources(b, zt), ra)

                    copy.start()

            loop(q, step_b)
            loop(q, step_a)

    def xb_copy(b, r):
        xx = (x + 1 + r) % p
        return remote(pb.at[b, z, xx], xrb.at[b, r], xb_s.at[b, r], xb_r.at[b, r], at_zx(z, xx))

    def stage_f1(b):
        for d in range(2):
            @pl.when(z != d * (q - 1))
            def _():
                ub_copy(d, b, z, udb.at[d, b, z]).wait_recv()
                loop(p, lambda xx: add_into(
                    pb.at[b, z, xx], [pb.at[b, z, xx], udb.at[d, b, z, xx]], rb))
        loop(p - 1, lambda r: xb_copy(b, r).start())

        wait_x(b, z)
        for d in range(2):
            @pl.when(z != d * (q - 1))
            def _():
                ud_copy(d, b, z).wait_recv()
        out = fin.at[b, pl.ds(0, ra)]

        @pl.when(z == 0)
        def _():
            add_into(out, x_sources(b, z) + [ud.at[1, b, z]], ra)

        @pl.when(z == q - 1)
        def _():
            add_into(out, x_sources(b, z) + [ud.at[0, b, z]], ra)

        @pl.when((z > 0) & (z < q - 1))
        def _():
            add_into(out, x_sources(b, z) + [ud.at[0, b, z], ud.at[1, b, z]], ra)

    def gh_copy(b):
        return remote(fin.at[b], gh_ref.at[n], gh_s.at[b], gh_r.at[b], (wi, twin(b)))

    def gh_here():
        return pltpu.make_async_copy(fin.at[0], gh_ref.at[n], l_sem.at[0])

    def stage_f2(b):
        loop(p - 1, lambda r: xb_copy(b, r).wait_recv())
        add_into(fin.at[b, pl.ds(ra, rb)],
                 [pb.at[b, z, x]] + [xrb.at[b, r] for r in range(p - 1)], rb)

        @pl.when(b == 0)
        def _():
            gh_here().start()

        @pl.when(b != 0)
        def _():
            gh_copy(b).start()

    def mz_copy(k, d, src):
        return remote(src, cols_ref.at[x, k], mz_s.at[d, k], mz_r.at[k], at_zx(z + 1 - 2 * d, x))

    def mx_copy(k, r, src):
        return remote(src, cols_ref.at[x, k], mx_s.at[k, r], mx_r.at[k, r], at_zx(z, (x + 1 + r) % p))

    def cols_here(k):
        return pltpu.make_async_copy(grads.at[k], cols_ref.at[x, k], w_sem.at[k])

    def multicast_source(k):
        @pl.when(z == n)
        def _():
            cols_here(k).start()
            for d in range(2):
                @pl.when(z != (1 - d) * (q - 1))
                def _():
                    mz_copy(k, d, grads.at[k]).start()

    def multicast_relay(k):
        @pl.when(z == n)
        def _():
            loop(p - 1, lambda r: mx_copy(k, r, grads.at[k]).start())

        for d in range(2):
            @pl.when((z - n) * (1 - 2 * d) > 0)
            def _():
                mz_copy(k, d, cols_ref.at[x, k]).wait_recv()

                @pl.when(z != (1 - d) * (q - 1))
                def _():
                    mz_copy(k, d, cols_ref.at[x, k]).start()

                loop(p - 1, lambda r: mx_copy(k, r, cols_ref.at[x, k]).start())

    def stage(s):
        @pl.when(s < q)
        def _():
            @pl.when(s == 1)
            def _():
                for k in range(1, q):
                    ag_copy(k).wait_recv()
                for k in range(q):
                    multicast_source(k)

            stage_x(s)

        @pl.when((s >= 1) & (s <= q))
        def _():
            stage_z(s - 1)
            @pl.when(s == 1)
            def _():
                for k in range(q // 2):
                    multicast_relay(k)

            @pl.when(s == 2)
            def _():
                for k in range(q // 2, q):
                    multicast_relay(k)

        @pl.when((s >= 2) & (s <= q + 1))
        def _():
            stage_f1(s - 2)

        @pl.when((s >= 3) & (s <= q + 2))
        def _():
            stage_f2(s - 3)

    loop(q + 3, stage)

    for k in range(1, q):
        ag_copy(k).wait_send()
        hid_copy(k).wait()
        gh_copy(k).wait()
    hid_here.wait()
    gh_here().wait()

    def drain_b(b):
        loop(p - 1, lambda r: xb_copy(b, r).wait_send())

        def per_row(zt):
            loop(p - 1, lambda r: xa_copy(b, zt, r).wait_send())
            for d in range(2):
                @pl.when((zt - z) * (1 - 2 * d) > 0)
                def _():
                    ud_copy(d, b, zt).wait_send()
                    ub_copy(d, b, zt, udb.at[d, b, zt]).wait_send()

        loop(q, per_row)

        @pl.when(z == n)
        def _():
            cols_here(b).wait()

        for d in range(2):
            @pl.when(((z - n) * (1 - 2 * d) >= 0) & (z != (1 - d) * (q - 1)))
            def _():
                mz_copy(b, d, cols_ref.at[x, b]).wait_send()
        loop(p - 1, lambda r: mx_copy(b, r, cols_ref.at[x, b]).wait())

    loop(q, drain_b)


def exchange(wide, narrow, hidden, grad_out, weight, scale_t):
    q = narrow
    p = wide // narrow
    tokens, features = grad_out.shape
    units = weight.shape[1]
    ra = tokens * 3 // 4 // 16 * 16
    rb = tokens - ra
    dma = pltpu.SemaphoreType.DMA
    any_space = pl.BlockSpec(memory_space=pl.ANY)
    vm = pl.BlockSpec(memory_space=pltpu.VMEM)
    return pl.pallas_call(
        functools.partial(exchange_kernel, q, p, ra),
        out_shape=(
            jax.ShapeDtypeStruct((narrow, tokens, units), BF16),
            jax.ShapeDtypeStruct((p, q, tokens, features), BF16),
            jax.ShapeDtypeStruct((q,) + hidden.shape, BF16),
        ),
        in_specs=[vm, any_space, any_space, any_space],
        out_specs=(any_space, any_space, any_space),
        scratch_shapes=[
            pltpu.VMEM((wide, units, features), BF16),
            pltpu.VMEM((scale_t.shape[1], features), F32),
            pltpu.VMEM((q, tokens, features), BF16),
            pltpu.VMEM(hidden.shape, BF16),
            pltpu.VMEM((q, q, p, ra, units), BF16),
            pltpu.VMEM((q, q, p, rb, units), BF16),
            pltpu.VMEM((q, q, p - 1, ra, units), BF16),
            pltpu.VMEM((2, q, q, ra, units), BF16),
            pltpu.VMEM((2, q, q, p, rb, units), BF16),
            pltpu.VMEM((q, p - 1, rb, units), BF16),
            pltpu.VMEM((q, tokens, units), BF16),
            dma((wide,)), dma((2,)), dma((q,)), dma((q,)), dma((q,)), dma((q,)),
            dma((q, q, p - 1)), dma((q, q, p - 1)),
            dma((2, q, q)), dma((2, q, q)), dma((2, q, q)), dma((2, q, q)),
            dma((q, p - 1)), dma((q, p - 1)), dma((q,)), dma((q,)),
            dma((2, q)), dma((q,)), dma((q, p - 1)), dma((q, p - 1)),
        ],
        compiler_params=pltpu.CompilerParams(
            collective_id=0, has_side_effects=True, vmem_limit_bytes=62 * 1024 * 1024),
        name="exchange",
    )(scale_t, weight, grad_out, hidden)


def outer_kernel(groups, units, cols_ref, hidden_ref, out_ref):
    for g in range(groups):
        part = lax.dot_general(
            cols_ref[0], hidden_ref[:, g * units:(g + 1) * units],
            (((0,), (0,)), ((), ())), preferred_element_type=F32)
        out_ref[:, g, :] = part.astype(BF16)


def outer_product(cols, hidden, groups):
    p, tokens, features = cols.shape
    units = hidden.shape[1] // groups
    rows = min(256, features)
    steps = features // rows
    return pl.pallas_call(
        functools.partial(outer_kernel, groups, units),
        grid=(p, steps),
        out_shape=jax.ShapeDtypeStruct((p * features, groups, units), BF16),
        in_specs=[
            pl.BlockSpec((1, tokens, rows), lambda i, j: (i, 0, j)),
            pl.BlockSpec(hidden.shape, lambda i, j: (0, 0), pipeline_mode=pl.Buffered(1)),
        ],
        out_specs=pl.BlockSpec((rows, groups, units), lambda i, j: (i * steps + j, 0, 0)),
        compiler_params=pltpu.CompilerParams(vmem_limit_bytes=60 * 1024 * 1024),
        name="outer_product",
    )(cols, hidden)


def per_device(wide, narrow, hidden, grad_out, weight_base, block_scale):
    tokens, groups, units = hidden.shape
    features = grad_out.shape[1]
    flat = hidden.reshape(tokens, groups * units)
    weight = weight_base.reshape(wide, weight_base.shape[0] // wide, features)
    gh, cols, hall = exchange(wide, narrow, flat, grad_out, weight, block_scale.T)
    grad_hidden = gh.transpose(1, 0, 2)
    p = cols.shape[0]
    every = narrow * tokens
    grad_weight = outer_product(
        cols.reshape(p, every, features), hall.reshape(every, groups * units), groups)
    return grad_hidden, grad_weight


def solution(mesh):
    wide, narrow = mesh.shape["wide"], mesh.shape["narrow"]
    return jax.shard_map(
        functools.partial(per_device, wide, narrow),
        mesh=mesh,
        in_specs=(P("narrow", None, "wide"), P("narrow", "wide"), P("narrow", "wide"), P("narrow", "wide")),
        out_specs=(P("narrow", None, "wide"), P("narrow", None, "wide")),
        check_vma=False,
    )
```

profile of v0, /device:TPU:0, one launch (start us, length us, event | category | flops | bytes accessed | tf_op | source)
XLA Modules:
  0.0 189.9 jit_solution(17726946434412317786)
XLA Ops:
  0.6 2.6 %copy.7 = bf16[16,8,4,1024]{3,1,2,0:T(8,128)(2,1)} copy(bf16[16,8,4,1024]{3,2,1,0:T(4,128)(2,1)} %bitcast.11) | data formatting | bytes 2097152
  3.2 162.0 %exchange.1 = (bf16[4,128,1024]{2,1,0:T(8,128)(2,1)}, bf16[2,4,128,1024]{3,2,1,0:T(8,128)(2,1)}, bf16[4,128,4096]{2,1,0:T(8,128)(2,1)}) custom-call(bf16[64,512]{1,0:T(8,128)(2,1)} %bitcast.13, bf16[8,1024,1024]{2,1,0:T(8,128)(2,1)} %bitcast.7, bf16[128,1024]{1,0:T(8,128)(2,1)} %grad_ref.1, bf16[128,4096]{1,0:T(8,128)(2,1)} %bitcast.8), custom_call_target="tpu_custom_call" | custom-call | tf_op jit(solution)/shard_map/exchange/pallas_call | solution.py:391
  165.2 3.0 %copy.6 = bf16[128,4,1024]{2,1,0:T(4,128)(2,1)} copy(bf16[128,4,1024]{2,0,1:T(8,128)(2,1)} %bitcast.12) | data formatting | bytes 2097152
  168.2 21.7 %outer_product.1 = bf16[2048,4,1024]{2,1,0:T(4,128)(2,1)} custom-call(bf16[2,512,1024]{2,1,0:T(8,128)(2,1)} %bitcast.10, bf16[512,4096]{1,0:T(8,128)(2,1)} %bitcast.9), custom_call_target="tpu_custom_call" | custom-call | tf_op jit(solution)/shard_map/outer_product/pallas_call | solution.py:437
where the time goes:
time: 190 us
  Pallas kernels  184 us (97%)
  local copies, waits for them, and re-layouts  5.58 us (3%)
    pallas_call x1, Pallas kernels, exchange(): pl.pallas_call(functools.partial(exchange_kernel, q, p, ra), out_shape=(j...  162 us
    pallas_call x1, Pallas kernels, outer_product(): pl.pallas_call(functools.partial(outer_kernel, groups, units), grid=(p, s...  21.7 us
    unnamed x2, local copies, waits for them, and re-layouts  5.58 us

commit v1 on v0

--- a/solution.py
+++ b/solution.py
@@ -13,12 +13,12 @@
 BF16 = jnp.bfloat16
 
 
-def loop(count, body):
+def loop(count, body, unroll=1):
     def step(i, carry):
         body(i)
         return carry
 
-    lax.fori_loop(0, count, step, 0)
+    lax.fori_loop(0, count, step, 0, unroll=unroll)
 
 
 def add_into(dst, sources, rows):
@@ -35,9 +35,9 @@
 def exchange_kernel(
     q, p, ra, scale_ref, weight_ref, grad_ref, hidden_ref,
     gh_ref, cols_ref, hall_ref,
-    weff, s32, grads, hid, pa, pb, xr, ud, udb, xrb, fin,
+    weff, s32, grads, raw, hid, pa, pb, xr, ud, udb, xrb, fin,
     w_sem, l_sem, ag_s, ag_r, hd_s, hd_r, xa_s, xa_r, ud_s, ud_r, ub_s, ub_r,
-    xb_s, xb_r, gh_s, gh_r, mz_s, mz_r, mx_s, mx_r,
+    xb_s, xb_r, gh_s, gh_r, mz_s, mz_r, mx_s, mx_r, own_sem,
 ):
     wide = q * p
     wi = lax.axis_index("wide")
@@ -49,9 +49,8 @@
     high = (2 * z) // q
 
     def twin(k):
-        a, b = n % 2, n // 2
-        ka, kb = k % 2, k // 2
-        return ((a + ka) % 2) + 2 * ((b + kb) % 2)
+        a, b = k // 2, (k % 2 + k // 2) % 2
+        return ((n % 2 + a) % 2) + 2 * ((n // 2 + b) % 2)
 
     def remote(src, dst, send, recv, to):
         return pltpu.make_async_remote_copy(
@@ -66,7 +65,7 @@
 
     own_grad = pltpu.make_async_copy(grad_ref, grads.at[0], l_sem.at[0])
     own_grad.start()
-    own_hid = pltpu.make_async_copy(hidden_ref, hid, l_sem.at[1])
+    own_hid = pltpu.make_async_copy(hidden_ref, raw, l_sem.at[1])
     own_hid.start()
 
     def weight_copy(c):
@@ -110,8 +109,25 @@
     def hid_copy(k):
         return remote(hid, hall_ref.at[k], hd_s.at[k], hd_r.at[k], (wi, twin(k)))
 
+    def hid_here():
+        return pltpu.make_async_copy(hid, hall_ref.at[0], l_sem.at[1])
+
+    def share_hidden():
+        own_hid.wait()
+        groups, width = raw.shape[1:]
+
+        def step(i):
+            at = pl.ds(pl.multiple_of(i * 16, 16), 16)
+            for g in range(groups):
+                hid[at, g * width:(g + 1) * width] = raw[at, g, :]
+
+        loop(raw.shape[0] // 16, step)
+        for k in range(1, q):
+            hid_copy(k).start()
+        hid_here().start()
+
     own_grad.wait()
-    for k in (2, 3, 1):
+    for k in range(1, q):
         ag_copy(k).start()
 
     features = weff.shape[2]
@@ -123,12 +139,6 @@
     s32[...] = lax.dot_general(
         scale_ref[...], spread, (((0,), (0,)), ((), ())), preferred_element_type=F32)
 
-    own_hid.wait()
-    for k in (2, 3, 1):
-        hid_copy(k).start()
-    hid_here = pltpu.make_async_copy(hid, hall_ref.at[0], l_sem.at[1])
-    hid_here.start()
-
     units = weff.shape[1]
     per_chunk = units // BLOCK
 
@@ -140,7 +150,7 @@
             factor = s32[pl.ds(c * per_chunk + i, 1), :]
             weff[c, at, :] = (weff[c, at, :].astype(F32) * factor).astype(BF16)
 
-        loop(per_chunk, step)
+        loop(per_chunk, step, 4)
 
     def xa_copy(b, zt, r):
         xx = (x + 1 + r) % p
@@ -154,31 +164,42 @@
         return remote(src, udb.at[d, b, zt], ub_s.at[d, b, zt], ub_r.at[d, b, zt],
                       at_zx(z + 1 - 2 * d, x))
 
-    def stage_x(b):
-        def per_row(i):
-            zt = order(i, high)
-
-            def per_col(xx):
-                c = zt * p + xx
-
-                @pl.when(b == 0)
-                def _():
-                    scale_chunk(c)
-
-                part = lax.dot_general(
-                    grads[b], weff[c], (((1,), (1,)), ((), ())), preferred_element_type=F32
-                ).astype(BF16)
-                pa[b, zt, xx] = part[:ra]
-                pb[b, zt, xx] = part[ra:]
-
-            loop(p, per_col)
-            loop(p - 1, lambda r: xa_copy(b, zt, r).start())
-            for d in range(2):
-                @pl.when((z == d * (q - 1)) & (zt != z))
-                def _():
-                    ub_copy(d, b, zt, pb.at[b, zt]).start()
-
-        loop(q, per_row)
+    def send_row(b, zt):
+        loop(p - 1, lambda r: xa_copy(b, zt, r).start())
+        for d in range(2):
+            @pl.when((z == d * (q - 1)) & (zt != z))
+            def _():
+                ub_copy(d, b, zt, pb.at[b, zt]).start()
+
+    def keep(b, zt, xx, part):
+        pa[b, zt, xx] = part[:ra]
+        pb[b, zt, xx] = part[ra:]
+
+    def first_rows(i):
+        zt = order(i, high)
+
+        def per_col(xx):
+            c = zt * p + xx
+            scale_chunk(c)
+            keep(0, zt, xx, lax.dot_general(
+                grads[0], weff[c], (((1,), (1,)), ((), ())), preferred_element_type=F32
+            ).astype(BF16))
+
+        loop(p, per_col)
+        send_row(0, zt)
+
+    def other_rows(i):
+        zt = order(i, high)
+
+        def per_col(xx):
+            part = lax.dot_general(
+                grads[1:].reshape((q - 1) * tokens, features), weff[zt * p + xx],
+                (((1,), (1,)), ((), ())), preferred_element_type=F32).astype(BF16)
+            for b in range(1, q):
+                keep(b, zt, xx, part[(b - 1) * tokens:b * tokens])
+
+        loop(p, per_col)
+        send_row(1, zt)
 
     def wait_x(b, zt):
         loop(p - 1, lambda r: xa_copy(b, zt, r).wait_recv())
@@ -186,16 +207,14 @@
     def x_sources(b, zt):
         return [pa.at[b, zt, x]] + [xr.at[b, zt, r] for r in range(p - 1)]
 
-    def stage_z(b):
+    def stage_zb(b):
         for ph in range(2):
             d = (ph + high) % 2
-            sign = 1 - 2 * d
-            edge = d * (q - 1)
 
             def step_b(i):
                 zt = order(i, d)
 
-                @pl.when(((zt - z) * sign > 0) & (z != edge))
+                @pl.when(((zt - z) * (1 - 2 * d) > 0) & (z != d * (q - 1)))
                 def _():
                     copy = ub_copy(d, b, zt, udb.at[d, b, zt])
                     copy.wait_recv()
@@ -203,10 +222,17 @@
                         udb.at[d, b, zt, xx], [udb.at[d, b, zt, xx], pb.at[b, zt, xx]], rb))
                     copy.start()
 
+            loop(q, step_b)
+
+    def stage_za(b):
+        for ph in range(2):
+            d = (ph + high) % 2
+            edge = d * (q - 1)
+
             def step_a(i):
                 zt = order(i, d)
 
-                @pl.when((zt - z) * sign > 0)
+                @pl.when((zt - z) * (1 - 2 * d) > 0)
                 def _():
                     wait_x(b, zt)
                     copy = ud_copy(d, b, zt)
@@ -222,7 +248,6 @@
 
                     copy.start()
 
-            loop(q, step_b)
             loop(q, step_a)
 
     def xb_copy(b, r):
@@ -283,7 +308,7 @@
         return remote(src, cols_ref.at[x, k], mx_s.at[k, r], mx_r.at[k, r], at_zx(z, (x + 1 + r) % p))
 
     def cols_here(k):
-        return pltpu.make_async_copy(grads.at[k], cols_ref.at[x, k], w_sem.at[k])
+        return pltpu.make_async_copy(grads.at[k], cols_ref.at[x, k], own_sem.at[k])
 
     def multicast_source(k):
         @pl.when(z == n)
@@ -310,46 +335,41 @@
 
                 loop(p - 1, lambda r: mx_copy(k, r, cols_ref.at[x, k]).start())
 
-    def stage(s):
-        @pl.when(s < q)
-        def _():
-            @pl.when(s == 1)
-            def _():
-                for k in range(1, q):
-                    ag_copy(k).wait_recv()
-                for k in range(q):
-                    multicast_source(k)
-
-            stage_x(s)
-
-        @pl.when((s >= 1) & (s <= q))
-        def _():
-            stage_z(s - 1)
-            @pl.when(s == 1)
-            def _():
-                for k in range(q // 2):
-                    multicast_relay(k)
-
-            @pl.when(s == 2)
-            def _():
-                for k in range(q // 2, q):
-                    multicast_relay(k)
-
-        @pl.when((s >= 2) & (s <= q + 1))
-        def _():
-            stage_f1(s - 2)
-
-        @pl.when((s >= 3) & (s <= q + 2))
-        def _():
-            stage_f2(s - 3)
-
-    loop(q + 3, stage)
+    multicast_source(0)
+    ag_copy(q - 1).wait_recv()
+    multicast_source(q - 1)
+    loop(q, first_rows)
+    for k in range(1, q - 1):
+        ag_copy(k).wait_recv()
+        multicast_source(k)
+    loop(q, other_rows)
+    loop(q - 2, lambda b: loop(q, lambda i: send_row(b + 2, order(i, high))))
+    share_hidden()
+    loop(q, stage_zb)
+
+    away = (z - n) * (z - n)
+    inner = jnp.logical_not(ends)
+
+    def relay_when(condition):
+        @pl.when(condition)
+        def _():
+            loop(q, multicast_relay)
+
+    relay_when((away == 0) | (inner & (away == 1)))
+    loop(2, stage_za)
+    relay_when(inner & (away > 1))
+    loop(q - 2, lambda b: stage_za(b + 2))
+    relay_when(ends & (away > 0))
+    loop(q - 1, stage_f1)
+    loop(q - 1, stage_f2)
+    stage_f1(q - 1)
+    stage_f2(q - 1)
 
     for k in range(1, q):
         ag_copy(k).wait_send()
         hid_copy(k).wait()
         gh_copy(k).wait()
-    hid_here.wait()
+    hid_here().wait()
     gh_here().wait()
 
     def drain_b(b):
@@ -385,6 +405,7 @@
     units = weight.shape[1]
     ra = tokens * 3 // 4 // 16 * 16
     rb = tokens - ra
+    flat = (tokens, hidden.shape[1] * hidden.shape[2])
     dma = pltpu.SemaphoreType.DMA
     any_space = pl.BlockSpec(memory_space=pl.ANY)
     vm = pl.BlockSpec(memory_space=pltpu.VMEM)
@@ -393,7 +414,7 @@
         out_shape=(
             jax.ShapeDtypeStruct((narrow, tokens, units), BF16),
             jax.ShapeDtypeStruct((p, q, tokens, features), BF16),
-            jax.ShapeDtypeStruct((q,) + hidden.shape, BF16),
+            jax.ShapeDtypeStruct((q,) + flat, BF16),
         ),
         in_specs=[vm, any_space, any_space, any_space],
         out_specs=(any_space, any_space, any_space),
@@ -402,6 +423,7 @@
             pltpu.VMEM((scale_t.shape[1], features), F32),
             pltpu.VMEM((q, tokens, features), BF16),
             pltpu.VMEM(hidden.shape, BF16),
+            pltpu.VMEM(flat, BF16),
             pltpu.VMEM((q, q, p, ra, units), BF16),
             pltpu.VMEM((q, q, p, rb, units), BF16),
             pltpu.VMEM((q, q, p - 1, ra, units), BF16),
@@ -413,7 +435,7 @@
             dma((q, q, p - 1)), dma((q, q, p - 1)),
             dma((2, q, q)), dma((2, q, q)), dma((2, q, q)), dma((2, q, q)),
             dma((q, p - 1)), dma((q, p - 1)), dma((q,)), dma((q,)),
-            dma((2, q)), dma((q,)), dma((q, p - 1)), dma((q, p - 1)),
+            dma((2, q)), dma((q,)), dma((q, p - 1)), dma((q, p - 1)), dma((q,)),
         ],
         compiler_params=pltpu.CompilerParams(
             collective_id=0, has_side_effects=True, vmem_limit_bytes=62 * 1024 * 1024),
@@ -421,44 +443,57 @@
     )(scale_t, weight, grad_out, hidden)
 
 
-def outer_kernel(groups, units, cols_ref, hidden_ref, out_ref):
+def outer_kernel(groups, units, cols_ref, hidden_ref, gh_ref, out_ref, grad_hidden_ref, rows_ref):
+    rows = cols_ref.shape[2]
     for g in range(groups):
         part = lax.dot_general(
             cols_ref[0], hidden_ref[:, g * units:(g + 1) * units],
             (((0,), (0,)), ((), ())), preferred_element_type=F32)
-        out_ref[:, g, :] = part.astype(BF16)
-
-
-def outer_product(cols, hidden, groups):
+        for j in range(units // 128):
+            rows_ref[j, pl.ds(g, rows, stride=groups), :] = part[:, j * 128:(j + 1) * 128]
+    for j in range(units // 128):
+        out_ref[:, :, j * 128:(j + 1) * 128] = rows_ref[j].astype(BF16).reshape(rows, groups, 128)
+    for g in range(groups):
+        grad_hidden_ref[:, g, :] = gh_ref[g]
+
+
+def outer_product(cols, hidden, gh):
     p, tokens, features = cols.shape
-    units = hidden.shape[1] // groups
+    groups, own, units = gh.shape
     rows = min(256, features)
     steps = features // rows
+    share = own // (p * steps)
     return pl.pallas_call(
         functools.partial(outer_kernel, groups, units),
         grid=(p, steps),
-        out_shape=jax.ShapeDtypeStruct((p * features, groups, units), BF16),
+        out_shape=(
+            jax.ShapeDtypeStruct((p * features, groups, units), BF16),
+            jax.ShapeDtypeStruct((own, groups, units), BF16),
+        ),
         in_specs=[
             pl.BlockSpec((1, tokens, rows), lambda i, j: (i, 0, j)),
             pl.BlockSpec(hidden.shape, lambda i, j: (0, 0), pipeline_mode=pl.Buffered(1)),
+            pl.BlockSpec((groups, share, units), lambda i, j: (0, i * steps + j, 0)),
         ],
-        out_specs=pl.BlockSpec((rows, groups, units), lambda i, j: (i * steps + j, 0, 0)),
+        out_specs=(
+            pl.BlockSpec((rows, groups, units), lambda i, j: (i * steps + j, 0, 0)),
+            pl.BlockSpec((share, groups, units), lambda i, j: (i * steps + j, 0, 0)),
+        ),
+        scratch_shapes=[pltpu.VMEM((units // 128, rows * groups, 128), F32)],
         compiler_params=pltpu.CompilerParams(vmem_limit_bytes=60 * 1024 * 1024),
         name="outer_product",
-    )(cols, hidden)
+    )(cols, hidden, gh)
 
 
 def per_device(wide, narrow, hidden, grad_out, weight_base, block_scale):
     tokens, groups, units = hidden.shape
     features = grad_out.shape[1]
-    flat = hidden.reshape(tokens, groups * units)
     weight = weight_base.reshape(wide, weight_base.shape[0] // wide, features)
-    gh, cols, hall = exchange(wide, narrow, flat, grad_out, weight, block_scale.T)
-    grad_hidden = gh.transpose(1, 0, 2)
+    gh, cols, hall = exchange(wide, narrow, hidden, grad_out, weight, block_scale.T)
     p = cols.shape[0]
     every = narrow * tokens
-    grad_weight = outer_product(
-        cols.reshape(p, every, features), hall.reshape(every, groups * units), groups)
+    grad_weight, grad_hidden = outer_product(
+        cols.reshape(p, every, features), hall.reshape(every, groups * units), gh)
     return grad_hidden, grad_weight
 
 

time: 190 us -> 142 us (0.75)
  Pallas kernels: 184 us -> 141 us
  local copies, waits for them, and re-layouts: 5.58 us -> 0 us
    pallas_call x1, Pallas kernels: 162 us -> 122 us  [exchange(): pl.pallas_call(functools.partial(exchange_kernel, q, p, ra), out_shape=(j...]
    unnamed x2 -> x0, local copies, waits for them, and re-layouts: 5.58 us -> none
where the time goes in v1:
time: 142 us
  Pallas kernels  141 us (99%)
    pallas_call x1, Pallas kernels, exchange(): pl.pallas_call(functools.partial(exchange_kernel, q, p, ra), out_shape=(j...  122 us
    pallas_call x1, Pallas kernels, outer_product(): pl.pallas_call(functools.partial(outer_kernel, groups, units), grid=(p, s...  19.9 us

profile of v1, /device:TPU:0, one launch (start us, length us, event | category | flops | bytes accessed | tf_op | source)
XLA Modules:
  0.0 142.1 jit_solution(4907477090985274310)
XLA Ops:
  0.6 121.5 %exchange.1 = (bf16[4,128,1024]{2,1,0:T(8,128)(2,1)}, bf16[2,4,128,1024]{3,2,1,0:T(8,128)(2,1)}, bf16[4,128,4096]{2,1,0:T(8,128)(2,1)}) custom-call(bf16[64,512]{1,0:T(8,128)(2,1)} %bitcast.7, bf16[8,1024,1024]{2,1,0:T(8,128)(2,1)} %bitcast.4, bf16[128,1024]{1,0:T(8,128)(2,1)} %grad_ref.1, bf16[128,4,1024]{2,1,0:T(4,128)(2,1)} %hidden_ref.1), custom_call_target="tpu_custom_call" | custom-call | tf_op jit(solution)/shard_map/exchange/pallas_call | solution.py:412
  122.2 19.9 %outer_product.1 = (bf16[2048,4,1024]{2,1,0:T(4,128)(2,1)}, bf16[128,4,1024]{2,1,0:T(4,128)(2,1)}) custom-call(bf16[2,512,1024]{2,1,0:T(8,128)(2,1)} %bitcast.6, bf16[512,4096]{1,0:T(8,128)(2,1)} %bitcast.5, bf16[4,128,1024]{2,1,0:T(8,128)(2,1)} %get-tuple-element.9.gh_ref), custom_call_target="tpu_custom_call" | custom-call | tf_op jit(solution)/shard_map/outer_product/pallas_call | solution.py:466

commit v2 on v1

--- a/solution.py
+++ b/solution.py
@@ -282,24 +282,33 @@
         def _():
             add_into(out, x_sources(b, z) + [ud.at[0, b, z], ud.at[1, b, z]], ra)
 
-    def gh_copy(b):
-        return remote(fin.at[b], gh_ref.at[n], gh_s.at[b], gh_r.at[b], (wi, twin(b)))
-
-    def gh_here():
-        return pltpu.make_async_copy(fin.at[0], gh_ref.at[n], l_sem.at[0])
+        share_out(b, 0)
+
+    def fin_part(b, half):
+        return fin.at[b, pl.ds(half * ra, rb if half else ra)]
+
+    def gh_part(half):
+        return gh_ref.at[n, pl.ds(half * ra, rb if half else ra)]
+
+    def gh_copy(b, half):
+        return remote(fin_part(b, half), gh_part(half), gh_s.at[half, b], gh_r.at[half, b], (wi, twin(b)))
+
+    def gh_here(half):
+        return pltpu.make_async_copy(fin_part(0, half), gh_part(half), gh_s.at[half, 0])
+
+    def share_out(b, half):
+        @pl.when(b == 0)
+        def _():
+            gh_here(half).start()
+
+        @pl.when(b != 0)
+        def _():
+            gh_copy(b, half).start()
 
     def stage_f2(b):
         loop(p - 1, lambda r: xb_copy(b, r).wait_recv())
-        add_into(fin.at[b, pl.ds(ra, rb)],
-                 [pb.at[b, z, x]] + [xrb.at[b, r] for r in range(p - 1)], rb)
-
-        @pl.when(b == 0)
-        def _():
-            gh_here().start()
-
-        @pl.when(b != 0)
-        def _():
-            gh_copy(b).start()
+        add_into(fin_part(b, 1), [pb.at[b, z, x]] + [xrb.at[b, r] for r in range(p - 1)], rb)
+        share_out(b, 1)
 
     def mz_copy(k, d, src):
         return remote(src, cols_ref.at[x, k], mz_s.at[d, k], mz_r.at[k], at_zx(z + 1 - 2 * d, x))
@@ -345,22 +354,46 @@
     loop(q, other_rows)
     loop(q - 2, lambda b: loop(q, lambda i: send_row(b + 2, order(i, high))))
     share_hidden()
-    loop(q, stage_zb)
-
     away = (z - n) * (z - n)
     inner = jnp.logical_not(ends)
-
-    def relay_when(condition):
+    near = (away == 0) | (inner & (away == 1))
+
+    def relay_early(condition):
         @pl.when(condition)
         def _():
-            loop(q, multicast_relay)
-
-    relay_when((away == 0) | (inner & (away == 1)))
-    loop(2, stage_za)
-    relay_when(inner & (away > 1))
-    loop(q - 2, lambda b: stage_za(b + 2))
-    relay_when(ends & (away > 0))
-    loop(q - 1, stage_f1)
+            loop(2, lambda i: multicast_relay(i * (q - 1)))
+
+    def relay_late(condition):
+        @pl.when(condition)
+        def _():
+            loop(q - 2, lambda i: multicast_relay(i + 1))
+
+    relay_early(near)
+    loop(q, stage_zb)
+    relay_late(near)
+    relay_early(inner & (away > 1))
+
+    def stage(s):
+        stage_za(s)
+        relay_late((s == 1) & inner & (away > 1))
+
+        @pl.when(inner & (s >= 1))
+        def _():
+            stage_f1(s - 1)
+
+    loop(q, stage)
+    relay_early(ends & (away > 0))
+
+    @pl.when(ends)
+    def _():
+        loop(q - 2, stage_f1)
+
+    relay_late(ends & (away > 0))
+
+    @pl.when(ends)
+    def _():
+        stage_f1(q - 2)
+
     loop(q - 1, stage_f2)
     stage_f1(q - 1)
     stage_f2(q - 1)
@@ -368,9 +401,11 @@
     for k in range(1, q):
         ag_copy(k).wait_send()
         hid_copy(k).wait()
-        gh_copy(k).wait()
+        for half in range(2):
+            gh_copy(k, half).wait()
     hid_here().wait()
-    gh_here().wait()
+    for half in range(2):
+        gh_here(half).wait()
 
     def drain_b(b):
         loop(p - 1, lambda r: xb_copy(b, r).wait_send())
@@ -434,7 +469,7 @@
             dma((wide,)), dma((2,)), dma((q,)), dma((q,)), dma((q,)), dma((q,)),
             dma((q, q, p - 1)), dma((q, q, p - 1)),
             dma((2, q, q)), dma((2, q, q)), dma((2, q, q)), dma((2, q, q)),
-            dma((q, p - 1)), dma((q, p - 1)), dma((q,)), dma((q,)),
+            dma((q, p - 1)), dma((q, p - 1)), dma((2, q)), dma((2, q)),
             dma((2, q)), dma((q,)), dma((q, p - 1)), dma((q, p - 1)), dma((q,)),
         ],
         compiler_params=pltpu.CompilerParams(

time: 142 us -> 132 us (0.930)
  Pallas kernels: 141 us -> 131 us
    pallas_call x1, Pallas kernels: 122 us -> 111 us  [exchange(): pl.pallas_call(functools.partial(exchange_kernel, q, p, ra), out_shape=(j...]
where the time goes in v2:
time: 132 us
  Pallas kernels  131 us (99%)
    pallas_call x1, Pallas kernels, exchange(): pl.pallas_call(functools.partial(exchange_kernel, q, p, ra), out_shape=(j...  111 us
    pallas_call x1, Pallas kernels, outer_product(): pl.pallas_call(functools.partial(outer_kernel, groups, units), grid=(p, s...  19.9 us

profile of v2, /device:TPU:0, one launch (start us, length us, event | category | flops | bytes accessed | tf_op | source)
XLA Modules:
  0.0 131.7 jit_solution(13713337335142842688)
XLA Ops:
  0.6 111.2 %exchange.1 = (bf16[4,128,1024]{2,1,0:T(8,128)(2,1)}, bf16[2,4,128,1024]{3,2,1,0:T(8,128)(2,1)}, bf16[4,128,4096]{2,1,0:T(8,128)(2,1)}) custom-call(bf16[64,512]{1,0:T(8,128)(2,1)} %bitcast.7, bf16[8,1024,1024]{2,1,0:T(8,128)(2,1)} %bitcast.4, bf16[128,1024]{1,0:T(8,128)(2,1)} %grad_ref.1, bf16[128,4,1024]{2,1,0:T(4,128)(2,1)} %hidden_ref.1), custom_call_target="tpu_custom_call" | custom-call | tf_op jit(solution)/shard_map/exchange/pallas_call | solution.py:447
  111.9 19.9 %outer_product.1 = (bf16[2048,4,1024]{2,1,0:T(4,128)(2,1)}, bf16[128,4,1024]{2,1,0:T(4,128)(2,1)}) custom-call(bf16[2,512,1024]{2,1,0:T(8,128)(2,1)} %bitcast.6, bf16[512,4096]{1,0:T(8,128)(2,1)} %bitcast.5, bf16[4,128,1024]{2,1,0:T(8,128)(2,1)} %get-tuple-element.9.gh_ref), custom_call_target="tpu_custom_call" | custom-call | tf_op jit(solution)/shard_map/outer_product/pallas_call | solution.py:501

commit v3 on v2

--- a/solution.py
+++ b/solution.py
@@ -164,13 +164,16 @@
         return remote(src, udb.at[d, b, zt], ub_s.at[d, b, zt], ub_r.at[d, b, zt],
                       at_zx(z + 1 - 2 * d, x))
 
-    def send_row(b, zt):
-        loop(p - 1, lambda r: xa_copy(b, zt, r).start())
+    def send_ends(b, zt):
         for d in range(2):
             @pl.when((z == d * (q - 1)) & (zt != z))
             def _():
                 ub_copy(d, b, zt, pb.at[b, zt]).start()
 
+    def send_row(b, zt):
+        loop(p - 1, lambda r: xa_copy(b, zt, r).start())
+        send_ends(b, zt)
+
     def keep(b, zt, xx, part):
         pa[b, zt, xx] = part[:ra]
         pb[b, zt, xx] = part[ra:]
@@ -178,15 +181,20 @@
     def first_rows(i):
         zt = order(i, high)
 
-        def per_col(xx):
+        def per_col(r):
+            xx = (x + 1 + r) % p
             c = zt * p + xx
             scale_chunk(c)
             keep(0, zt, xx, lax.dot_general(
                 grads[0], weff[c], (((1,), (1,)), ((), ())), preferred_element_type=F32
             ).astype(BF16))
 
+            @pl.when(r < p - 1)
+            def _():
+                xa_copy(0, zt, r).start()
+
         loop(p, per_col)
-        send_row(0, zt)
+        send_ends(0, zt)
 
     def other_rows(i):
         zt = order(i, high)

time: 132 us -> 133 us (level); the launches traced: 132 us -> 130 us
    pallas_call x1, Pallas kernels: 111 us -> 110 us  [exchange(): pl.pallas_call(functools.partial(exchange_kernel, q, p, ra), out_shape=(j...]
where the time goes in v3:
time: 133 us; the launch traced here: 130 us
  Pallas kernels  130 us (98%)
    pallas_call x1, Pallas kernels, exchange(): pl.pallas_call(functools.partial(exchange_kernel, q, p, ra), out_shape=(j...  110 us
    pallas_call x1, Pallas kernels, outer_product(): pl.pallas_call(functools.partial(outer_kernel, groups, units), grid=(p, s...  19.9 us

profile of v3, /device:TPU:0, one launch (start us, length us, event | category | flops | bytes accessed | tf_op | source)
XLA Modules:
  0.0 130.2 jit_solution(6740151552305264183)
XLA Ops:
  0.6 109.7 %exchange.1 = (bf16[4,128,1024]{2,1,0:T(8,128)(2,1)}, bf16[2,4,128,1024]{3,2,1,0:T(8,128)(2,1)}, bf16[4,128,4096]{2,1,0:T(8,128)(2,1)}) custom-call(bf16[64,512]{1,0:T(8,128)(2,1)} %bitcast.7, bf16[8,1024,1024]{2,1,0:T(8,128)(2,1)} %bitcast.4, bf16[128,1024]{1,0:T(8,128)(2,1)} %grad_ref.1, bf16[128,4,1024]{2,1,0:T(4,128)(2,1)} %hidden_ref.1), custom_call_target="tpu_custom_call" | custom-call | tf_op jit(solution)/shard_map/exchange/pallas_call | solution.py:455
  110.3 19.9 %outer_product.1 = (bf16[2048,4,1024]{2,1,0:T(4,128)(2,1)}, bf16[128,4,1024]{2,1,0:T(4,128)(2,1)}) custom-call(bf16[2,512,1024]{2,1,0:T(8,128)(2,1)} %bitcast.6, bf16[512,4096]{1,0:T(8,128)(2,1)} %bitcast.5, bf16[4,128,1024]{2,1,0:T(8,128)(2,1)} %get-tuple-element.9.gh_ref), custom_call_target="tpu_custom_call" | custom-call | tf_op jit(solution)/shard_map/outer_product/pallas_call | solution.py:509
